TPU v7x, 256 devices: a whole 4x4x8 slice. The times are simulated.
256 devices in a mesh: layer: 16 (over y, x_hi, core), row: 16 (over z, x_lo).
Axes of the slice: x: 4 (x_hi: 2, x_lo: 2; x = x_hi * 2 + x_lo), y: 4, z: 8, core: 2. Of those that a mesh axis runs over, the one named last changes fastest.
Arguments:
- magnet: float32 [3, 16, 1024, 1024], P(None, 'layer', 'row'), may hold values from -1 to 1, as said below
- saturation: float32 [16], P('layer'), may hold values from 0.5 to 2
- stiffness: float32 [16], P('layer'), may hold values from 0.1 to 0.4
- damping: float32 [16], P('layer'), may hold values from 0.02 to 0.5
- interface_sign: int32 [16, 2], P('layer'), may hold values from -1 to 1, as said below
Outputs:
- torque: float32 [3, 16, 1024, 1024], P(None, 'layer', 'row')
Inputs may be any that keep to these rules, and one draw needn't show every extreme that they name: `magnet`: the three components of every cell form a unit vector. Every entry is -1 or 1; interface_sign[l, 1] equals interface_sign[l + 1, 0], the sign of the interface between layers l and l + 1; interface_sign[0, 0] and interface_sign[15, 1] belong to no interface.
All inputs are finite; a program needn't handle non-finite values.
Results may differ from a plain program's by a relative error of at most 0.0003.
Values sent between devices are 32-bit elements; how exact they have to be, the bound alone decides.
A program may use at most 128 MiB of HBM per device.

v0:
```python
import functools
import math

import jax
import jax.numpy as jnp
import numpy as np
from jax import lax
from jax.experimental import pallas as pl
from jax.experimental.pallas import tpu as pltpu
from jax.sharding import PartitionSpec as P

N = 1024
HALF = N // 2
BINS = N // 4
LAYERS = 16
ROWS = 64
DEVICES = 256
THICKNESS = 1.0
LAYER_PITCH = 1.5
RKKY_STRENGTH = 0.8
F32 = jnp.float32
BF16 = jnp.bfloat16
NT = (((1,), (1,)), ((), ()))
NN = (((1,), (0,)), ((), ()))
TN = (((0,), (0,)), ((), ()))


def wave_tables():
    grid = np.arange(HALF)
    bins = np.arange(BINS)
    tables = []
    for parity in range(2):
        phase = (2 * bins[:, None] + parity) * grid[None, :] % N * (2.0 * np.pi / N)
        cosines, sines = np.cos(phase), np.sin(phase)
        if parity == 0:
            sines[0] = 1.0 - 2.0 * (grid % 2)
        tables.append(np.concatenate([cosines, sines], axis=0))
    exact = np.stack(tables)
    high = exact.astype(np.dtype(BF16))
    low = (exact - high.astype(np.float64)).astype(np.dtype(BF16))
    return jnp.asarray(high), jnp.asarray(low)


def split(value):
    high = value.astype(BF16)
    return high, (value - high.astype(F32)).astype(BF16)


def product(left, right, dims):
    (left_high, left_low), (right_high, right_low) = left, right
    dot = functools.partial(lax.dot_general, dimension_numbers=dims, preferred_element_type=F32)
    return dot(left_high, right_high) + (dot(left_high, right_low) + dot(left_low, right_high))


def lane_low(shape):
    return lax.broadcasted_iota(jnp.int32, shape, len(shape) - 1) < ROWS


def forward_x_kernel(sat_ref, stiff_ref, sign_ref, magnet_ref, high_ref, low_ref, out_ref):
    left, right = magnet_ref[:, :HALF], magnet_ref[:, HALF:]
    low_half = lane_low((DEVICES, 128))
    first = lax.broadcasted_iota(jnp.int32, (DEVICES, 128), 0) == 0
    for slot in range(2):
        folded = left - right if slot else left + right
        folded = jnp.concatenate([folded, folded[2 * ROWS :]], axis=0)
        waves = product((high_ref[slot], low_ref[slot]), split(folded), NT)
        cosine, sine = waves[:BINS], waves[BINS:]
        one, two = cosine[:, :128], sine[:, :128]
        if slot == 0:
            x_one, x_two = jnp.where(first, two, one), jnp.where(first, one, two)
        else:
            x_one, x_two = one, two
        out_ref[pl.ds(slot, DEVICES, stride=8), :] = jnp.where(low_half, x_one, -two)
        out_ref[pl.ds(2 + slot, DEVICES, stride=8), :] = jnp.where(low_half, x_two, one)
        out_ref[pl.ds(4 + slot, DEVICES, stride=8), :] = jnp.where(
            low_half, -sine[:, 128:], cosine[:, 128:]
        )
    even = lax.rem(lax.axis_index("row"), 2) == 0
    six = jnp.where(even, sat_ref[0], sign_ref[0, 0].astype(F32))
    seven = jnp.where(even, stiff_ref[0], sign_ref[0, 1].astype(F32))
    out_ref[pl.ds(6, DEVICES, stride=8), :] = jnp.full((DEVICES, 128), six, F32)
    out_ref[pl.ds(7, DEVICES, stride=8), :] = jnp.full((DEVICES, 128), seven, F32)


def symbols(device, parity, tile, sine):
    shape = (8, 128)
    row = lax.broadcasted_iota(jnp.int32, shape, 0)
    slot, word = row % 2, row // 2 % 2
    bin_y = 2 * (lax.broadcasted_iota(jnp.int32, shape, 1) + 128 * tile) + parity
    if sine and parity == 0:
        bin_y = jnp.where(bin_y == 0, HALF, bin_y)
    special = jnp.logical_and(device == 0, slot == 0)
    bin_x = jnp.where(special, jnp.where(word == 0, HALF, 0), 2 * device + slot)
    top_x, top_y = bin_x == HALF, bin_y == HALF
    wave_x = bin_x.astype(F32) * (2.0 * math.pi / N)
    wave_y = bin_y.astype(F32) * (2.0 * math.pi / N)
    square = wave_x * wave_x + wave_y * wave_y
    anchor = square == 0.0
    norm = jnp.sqrt(jnp.where(anchor, 1.0, square))
    unit_x = jnp.where(anchor, 0.0, wave_x / norm)
    unit_y = jnp.where(anchor, 0.0, wave_y / norm)
    depth = THICKNESS * norm
    series = 1.0 / 5040.0
    for divisor in (-720.0, 120.0, -24.0, 6.0, -2.0, 1.0):
        series = series * depth + 1.0 / divisor
    ratio = jnp.where(depth < 0.25, series, (1.0 - jnp.exp(-depth)) / depth)
    self_z = jnp.where(anchor, 1.0, ratio)
    near = jnp.where(
        anchor, 0.0, 0.5 * depth * ratio * ratio * jnp.exp(-norm * (LAYER_PITCH - THICKNESS))
    )
    step = jnp.exp(-LAYER_PITCH * norm)
    bend = 2.0 * jnp.cos(wave_x) + 2.0 * jnp.cos(wave_y) - 4.0
    scale_x = jnp.where(jnp.logical_or(bin_x == 0, top_x), 1.0, 2.0)
    scale_y = jnp.where(jnp.logical_or(bin_y == 0, top_y), 1.0, 2.0)
    scale = scale_x * scale_y * (1.0 / (N * N))
    return dict(
        x=jnp.where(top_x, 0.0, unit_x),
        y=jnp.where(top_y, 0.0, unit_y),
        top_x=jnp.where(top_x, -unit_x, 0.0),
        top_y=jnp.where(top_y, unit_y, 0.0),
        self_z=self_z,
        near=near,
        step=step,
        bend=bend * scale,
        scale=scale,
    )


def couple_kernel(in_ref, high_ref, low_ref, out_ref, spec_ref, field_ref, keep_ref, top_ref):
    device = lax.axis_index("layer") * LAYERS + lax.axis_index("row")
    low_half = lane_low((8, 128))
    rows = lax.broadcasted_iota(jnp.int32, (8, 128), 0)

    def tile_of(layer, block):
        return in_ref[pl.ds(pl.multiple_of((layer * LAYERS + block) * 8, 8), 8), :]

    def gather(layer, carry):
        for pair in range(4):
            plus, minus = [], []
            for block in (2 * pair, 2 * pair + 1):
                one, two = tile_of(layer, block), tile_of(layer, block + 8)
                plus.append(one + two)
                minus.append(one - two)
            for parity, (one, two) in enumerate((plus, minus)):
                columns = slice(128 * pair, 128 * pair + 128)
                at = pl.ds(pl.multiple_of(layer * 8, 8), 8)
                spec_ref[parity, 0, at, columns] = jnp.where(low_half, one, pltpu.roll(two, 64, 1))
                spec_ref[parity, 1, at, columns] = jnp.where(low_half, pltpu.roll(one, 64, 1), two)
        return carry

    lax.fori_loop(0, LAYERS, gather, 0)
    for parity in range(2):
        waves = product(
            split(spec_ref[parity].reshape(2 * 8 * LAYERS, HALF)),
            (high_ref[parity], low_ref[parity]),
            NT,
        )
        spec_ref[parity] = waves.reshape(2, 8 * LAYERS, HALF)

    def parameter(layer, block, row):
        return jnp.broadcast_to(in_ref[pl.ds((layer * LAYERS + block) * 8 + row, 1), :], (8, 128))

    for parity in range(2):
        for tile in range(2):
            cos_at = slice(128 * tile, 128 * tile + 128)
            sin_at = slice(BINS + 128 * tile, BINS + 128 * tile + 128)
            both = [
                (symbols(device, parity, tile, sine), at)
                for sine, at in ((False, cos_at), (True, sin_at))
            ]

            def load(layer, at):
                at_rows = slice(8 * layer, 8 * layer + 8)
                one, two = spec_ref[parity, 0, at_rows, at], spec_ref[parity, 1, at_rows, at]
                up = jnp.where(rows < 2, pltpu.roll(one, 4, 0), pltpu.roll(two, 6, 0))
                return one, two, up

            (cs, _), (ss, _) = both
            rise = [jnp.zeros((8, 128), F32)] * 2
            for layer in range(LAYERS):
                sat = parameter(layer, 0, 6)
                (xc, yc, zc), (xs, ys, zs) = load(layer, cos_at), load(layer, sin_at)
                along = (cs["x"] * xc + cs["y"] * ys, ss["x"] * xs - ss["y"] * yc)
                for part, (a, z) in enumerate(zip(along, (zc, zs))):
                    sym = both[part][0]
                    a, z = sat * a, sat * z
                    keep_ref[layer, part, 0] = (1.0 - sym["self_z"]) * a + rise[part]
                    keep_ref[layer, part, 1] = sym["self_z"] * z + rise[part]
                    keep_ref[layer, part, 2] = sym["near"] * (a - z)
                    rise[part] = sym["step"] * rise[part] + sym["near"] * (a + z)
            fall = [jnp.zeros((8, 128), F32)] * 2
            for layer in reversed(range(LAYERS)):
                psi, chi = [], []
                for part in range(2):
                    sym = both[part][0]
                    psi.append(keep_ref[layer, part, 0] + fall[part])
                    chi.append(keep_ref[layer, part, 1] - fall[part])
                    fall[part] = sym["step"] * fall[part] + keep_ref[layer, part, 2]
                stiff = parameter(layer, 0, 7)
                below = RKKY_STRENGTH * parameter(layer, 1, 6) if layer > 0 else None
                above = RKKY_STRENGTH * parameter(layer, 1, 7) if layer < LAYERS - 1 else None
                for part, (sym, at) in enumerate(both):
                    here = load(layer, at)
                    cross = cs["y"] * psi[1] if part == 0 else -ss["y"] * psi[0]
                    field = [-sym["x"] * psi[part], cross, -chi[part]]
                    pair = [0.0, 0.0, 0.0]
                    if below is not None:
                        pair = [p + below * v for p, v in zip(pair, load(layer - 1, at))]
                    if above is not None:
                        pair = [p + above * v for p, v in zip(pair, load(layer + 1, at))]
                    hx, hy, hz = (
                        sym["scale"] * (f + p) + (stiff * sym["bend"]) * v
                        for f, p, v in zip(field, pair, here)
                    )
                    at_rows = slice(8 * layer, 8 * layer + 8)
                    field_ref[parity, 0, at_rows, at] = jnp.where(rows < 4, hx, pltpu.roll(hz, 4, 0))
                    field_ref[parity, 1, at_rows, at] = jnp.where(rows < 4, hy, pltpu.roll(hz, 2, 0))

            def top():
                for part, (sym, at) in enumerate(both):
                    rise = jnp.zeros((8, 128), F32)
                    fall = rise
                    for layer in range(LAYERS):
                        sat = parameter(layer, 0, 6)
                        x, y, _ = load(layer, at)
                        e = sat * (sym["top_x"] * x + sym["top_y"] * y)
                        top_ref[layer, 0] = (1.0 - sym["self_z"]) * e + rise
                        top_ref[layer, 1] = sym["near"] * e
                        rise = sym["step"] * rise + sym["near"] * e
                    for layer in reversed(range(LAYERS)):
                        psi = sym["scale"] * (top_ref[layer, 0] + fall)
                        fall = sym["step"] * fall + top_ref[layer, 1]
                        at_rows = slice(8 * layer, 8 * layer + 8)
                        for half, key in enumerate(("top_x", "top_y")):
                            field_ref[parity, half, at_rows, at] -= jnp.where(
                                rows < 4, sym[key] * psi, 0.0
                            )

            if parity == 0 and tile == 0:
                top()
            else:
                pl.when(device == 0)(top)

    for parity in range(2):
        spec_ref[parity] = product(
            split(field_ref[parity].reshape(2 * 8 * LAYERS, HALF)),
            (high_ref[parity], low_ref[parity]),
            NN,
        ).reshape(2, 8 * LAYERS, HALF)

    def scatter(layer, carry):
        at = pl.ds(pl.multiple_of(layer * 8, 8), 8)
        for pair in range(4):
            columns = slice(128 * pair, 128 * pair + 128)
            even = [spec_ref[0, half, at, columns] for half in range(2)]
            odd = [spec_ref[1, half, at, columns] for half in range(2)]
            for far in range(2):
                one, two = (e - o if far else e + o for e, o in zip(even, odd))
                block = layer * LAYERS + 8 * far + 2 * pair
                out_ref[pl.ds(pl.multiple_of(block * 8, 8), 8), :] = jnp.where(
                    low_half, one, pltpu.roll(two, 64, 1)
                )
                out_ref[pl.ds(pl.multiple_of(block * 8 + 8, 8), 8), :] = jnp.where(
                    low_half, pltpu.roll(one, 64, 1), two
                )
        return carry

    lax.fori_loop(0, LAYERS, scatter, 0)


def torque_kernel(damping_ref, magnet_ref, in_ref, high_ref, low_ref, out_ref):
    low_half = lane_low((DEVICES, 128))
    first = lax.broadcasted_iota(jnp.int32, (DEVICES, 128), 0) == 0
    parts = []
    for slot in range(2):
        one = in_ref[pl.ds(slot, DEVICES, stride=8), :]
        two = in_ref[pl.ds(2 + slot, DEVICES, stride=8), :]
        up = in_ref[pl.ds(4 + slot, DEVICES, stride=8), :]
        if slot == 0:
            x_one, x_two = jnp.where(first, two, one), jnp.where(first, one, two)
        else:
            x_one, x_two = one, two
        cosine = jnp.concatenate(
            [jnp.where(low_half, x_one, two), pltpu.roll(up, 64, 1)], axis=1
        )
        sine = jnp.concatenate([jnp.where(low_half, x_two, -one), -up], axis=1)
        waves = jnp.concatenate([cosine, sine], axis=0)
        parts.append(product(split(waves), (high_ref[slot], low_ref[slot]), TN))
    damping = damping_ref[0]
    factor = -1.0 / (1.0 + damping * damping)
    for far in range(2):
        at = slice(HALF * far, HALF * far + HALF)
        field = parts[0] - parts[1] if far else parts[0] + parts[1]
        h = [field[ROWS * c : ROWS * c + ROWS] for c in range(3)]
        m = [magnet_ref[ROWS * c : ROWS * c + ROWS, at] for c in range(3)]
        p = [m[c - 2] * h[c - 1] - m[c - 1] * h[c - 2] for c in range(3)]
        for c in range(3):
            relax = m[c - 2] * p[c - 1] - m[c - 1] * p[c - 2]
            out_ref[ROWS * c : ROWS * c + ROWS, at] = factor * (p[c] + damping * relax)


def call(kernel, out, scratch, inputs, smem):
    spaces = [pltpu.SMEM] * smem + [pltpu.VMEM] * (len(inputs) - smem)
    return pl.pallas_call(
        kernel,
        out_shape=jax.ShapeDtypeStruct(out, F32),
        in_specs=[pl.BlockSpec(memory_space=space) for space in spaces],
        out_specs=pl.BlockSpec(memory_space=pltpu.VMEM),
        scratch_shapes=[pltpu.VMEM(shape, F32) for shape in scratch],
    )(*inputs)


def exchange(blocks):
    blocks = blocks.reshape(DEVICES, 8, 128)
    blocks = lax.all_to_all(blocks, ("layer", "row"), split_axis=0, concat_axis=0, tiled=True)
    return blocks.reshape(8 * DEVICES, 128)


def on_device(magnet, saturation, stiffness, damping, interface_sign):
    flat = magnet.reshape(3 * ROWS, N)
    high, low = wave_tables()
    buffer = (8 * DEVICES, 128)
    waves = call(
        forward_x_kernel, buffer, [], (saturation, stiffness, interface_sign, flat, high, low), 3
    )
    spectrum = (2, 2, 8 * LAYERS, HALF)
    fields = call(
        couple_kernel,
        buffer,
        [spectrum, spectrum, (LAYERS, 2, 3, 8, 128), (LAYERS, 2, 8, 128)],
        (exchange(waves), high, low),
        0,
    )
    torque = call(
        torque_kernel, flat.shape, [], (damping, flat, exchange(fields), high, low), 1
    )
    return torque.reshape(magnet.shape)


def solution(mesh):
    in_specs = (P(None, "layer", "row", None), P("layer"), P("layer"), P("layer"), P("layer", None))
    out_specs = P(None, "layer", "row", None)
    return jax.shard_map(
        on_device, mesh=mesh, in_specs=in_specs, out_specs=out_specs, check_vma=False
    )
```

profile of v0, /device:TPU:1, one launch (start us, length us, event | category | flops | bytes accessed | tf_op | source)
XLA Modules:
  0.0 104.1 jit_solution(7691184222308931665)
XLA Ops:
  1.3 4.0 %shard_map.73 = f32[2048,128]{1,0:T(8,128)} custom-call(f32[1]{0:T(128)S(6)} %copy.9.sat_ref, f32[1]{0:T(128)S(6)} %copy.10.stiff_ref, s32[1,2]{1,0:T(1,128)} %sign_ref.1, f32[192,1024]{1,0:T(8,128)} %bitcast.12, bf16[2,512,512]{2,1,0:T(8,128)(2,1)} %constant.4.clone.high_ref, bf16[2,512,512]{2,1,0:T(8,128)(2,1)} %constant.5.clone.low_ref), custom_call_target="tpu_custom_call" | custom-call | tf_op jit(solution)/shard_map/pallas_call | solution.py:304
  5.2 47.5 %all_to_all.10 = f32[256,8,128]{2,1,0:T(8,128)} all-to-all(f32[256,8,128]{2,1,0:T(8,128)} %bitcast.9), channel_id=1, replica_groups=mesh['layer'=16,'row'=16] {'layer','row'}, dimensions={0} | all-to-all | bytes 2097152 | tf_op jit(solution)/shard_map/all_to_all | solution.py:315
  52.7 8.8 %shard_map.74 = f32[2048,128]{1,0:T(8,128)} custom-call(f32[2048,128]{1,0:T(8,128)} %bitcast.11, bf16[2,512,512]{2,1,0:T(8,128)(2,1)} %constant.4.clone.high_ref, bf16[2,512,512]{2,1,0:T(8,128)(2,1)} %constant.5.clone.low_ref), custom_call_target="tpu_custom_call" | custom-call | tf_op jit(solution)/shard_map/pallas_call | solution.py:304
  61.5 5.6 %all-to-all-start.1 = ((f32[256,8,128]{2,1,0:T(8,128)}), f32[256,8,128]{2,1,0:T(8,128)S(1)}, u32[]{:S(2)}, u32[]{:S(2)}) async-start(f32[256,8,128]{2,1,0:T(8,128)} %bitcast.10), calls=%async_computation.1 | async-start | bytes 2097152 | tf_op jit(solution)/shard_map/all_to_all | solution.py:315
  67.7 31.1 %all-to-all-done.1 = f32[256,8,128]{2,1,0:T(8,128)S(1)} async-done(((f32[256,8,128]{2,1,0:T(8,128)}), f32[256,8,128]{2,1,0:T(8,128)S(1)}, u32[]{:S(2)}, u32[]{:S(2)}) %all-to-all-start.1) | async-done | bytes 1048608 | tf_op jit(solution)/shard_map/all_to_all | solution.py:315
  98.8 0.0 copy-start
  98.8 1.0 copy-done
  99.8 4.3 %shard_map.75 = f32[192,1024]{1,0:T(8,128)} custom-call(f32[1]{0:T(128)S(6)} %copy.11.damping_ref, f32[192,1024]{1,0:T(8,128)} %bitcast.13, f32[2048,128]{1,0:T(8,128)} %bitcast.8, bf16[2,512,512]{2,1,0:T(8,128)(2,1)} %constant.4.clone.high_ref, bf16[2,512,512]{2,1,0:T(8,128)(2,1)} %constant.5.clone.low_ref), custom_call_target="tpu_custom_call" | custom-call | tf_op jit(solution)/shard_map/pallas_call | solution.py:304
Async XLA Ops:
  61.5 37.3 %all-to-all-start.1 = ((f32[256,8,128]{2,1,0:T(8,128)}), f32[256,8,128]{2,1,0:T(8,128)S(1)}, u32[]{:S(2)}, u32[]{:S(2)}) async-start(f32[256,8,128]{2,1,0:T(8,128)} %bitcast.10), calls=%async_computation.1 | async-start | bytes 2097152 | tf_op jit(solution)/shard_map/all_to_all | solution.py:315
  98.8 1.0 copy-start
where the time goes:
time: 104 us
  blocking collectives  47.5 us (46%)
  waiting for transfers between devices  31.1 us (30%)
  Pallas kernels  17.1 us (16%)
  starting transfers between devices  5.58 us (5%)
  between operations  1.95 us (2%)
    all_to_all x1, blocking collectives, exchange(): lax.all_to_all(blocks, ('layer', 'row'), split_axis=0, concat_axis=0, til...  47.5 us
    all_to_all x1, waiting for transfers between devices, exchange(): lax.all_to_all(blocks, ('layer', 'row'), split_axis=0, concat_axis=0, til...  31.1 us
    pallas_call x3, Pallas kernels, call(): pl.pallas_call(kernel, out_shape=jax.ShapeDtypeStruct(out, F32), in_specs...  17.1 us
    all_to_all x1, starting transfers between devices, exchange(): lax.all_to_all(blocks, ('layer', 'row'), split_axis=0, concat_axis=0, til...  5.58 us
  transfers between devices with their start and end apart: 1, of which 1 were waited for; matrix products, arithmetic and copies ran while one was open for 0% of the time, Pallas kernels for 0%

commit v1 on v0

--- a/solution.py
+++ b/solution.py
@@ -23,6 +23,8 @@
 NT = (((1,), (1,)), ((), ()))
 NN = (((1,), (0,)), ((), ()))
 TN = (((0,), (0,)), ((), ()))
+USED = 6
+MESH = pl.DeviceIdType.MESH
 
 
 def wave_tables():
@@ -56,30 +58,24 @@
     return lax.broadcasted_iota(jnp.int32, shape, len(shape) - 1) < ROWS
 
 
-def forward_x_kernel(sat_ref, stiff_ref, sign_ref, magnet_ref, high_ref, low_ref, out_ref):
+def forward_x(magnet_ref, high_ref, low_ref, out_ref, slot):
     left, right = magnet_ref[:, :HALF], magnet_ref[:, HALF:]
     low_half = lane_low((DEVICES, 128))
-    first = lax.broadcasted_iota(jnp.int32, (DEVICES, 128), 0) == 0
-    for slot in range(2):
-        folded = left - right if slot else left + right
-        folded = jnp.concatenate([folded, folded[2 * ROWS :]], axis=0)
-        waves = product((high_ref[slot], low_ref[slot]), split(folded), NT)
-        cosine, sine = waves[:BINS], waves[BINS:]
-        one, two = cosine[:, :128], sine[:, :128]
-        if slot == 0:
-            x_one, x_two = jnp.where(first, two, one), jnp.where(first, one, two)
-        else:
-            x_one, x_two = one, two
-        out_ref[pl.ds(slot, DEVICES, stride=8), :] = jnp.where(low_half, x_one, -two)
-        out_ref[pl.ds(2 + slot, DEVICES, stride=8), :] = jnp.where(low_half, x_two, one)
-        out_ref[pl.ds(4 + slot, DEVICES, stride=8), :] = jnp.where(
-            low_half, -sine[:, 128:], cosine[:, 128:]
-        )
-    even = lax.rem(lax.axis_index("row"), 2) == 0
-    six = jnp.where(even, sat_ref[0], sign_ref[0, 0].astype(F32))
-    seven = jnp.where(even, stiff_ref[0], sign_ref[0, 1].astype(F32))
-    out_ref[pl.ds(6, DEVICES, stride=8), :] = jnp.full((DEVICES, 128), six, F32)
-    out_ref[pl.ds(7, DEVICES, stride=8), :] = jnp.full((DEVICES, 128), seven, F32)
+    folded = left - right if slot else left + right
+    folded = jnp.concatenate([folded, folded[2 * ROWS :]], axis=0)
+    waves = product((high_ref[slot], low_ref[slot]), split(folded), NT)
+    cosine, sine = waves[:BINS], waves[BINS:]
+    one, two = cosine[:, :128], sine[:, :128]
+    if slot == 0:
+        first = lax.broadcasted_iota(jnp.int32, (DEVICES, 128), 0) == 0
+        x_one, x_two = jnp.where(first, two, one), jnp.where(first, one, two)
+    else:
+        x_one, x_two = one, two
+    out_ref[pl.ds(slot, DEVICES, stride=8), :] = jnp.where(low_half, x_one, -two)
+    out_ref[pl.ds(2 + slot, DEVICES, stride=8), :] = jnp.where(low_half, x_two, one)
+    out_ref[pl.ds(4 + slot, DEVICES, stride=8), :] = jnp.where(
+        low_half, -sine[:, 128:], cosine[:, 128:]
+    )
 
 
 def symbols(device, parity, tile, sine):
@@ -126,7 +122,7 @@
     )
 
 
-def couple_kernel(in_ref, high_ref, low_ref, out_ref, spec_ref, field_ref, keep_ref, top_ref):
+def couple(in_ref, high_ref, low_ref, out_ref, trait_ref, spec_ref, field_ref, keep_ref, top_ref):
     device = lax.axis_index("layer") * LAYERS + lax.axis_index("row")
     low_half = lane_low((8, 128))
     rows = lax.broadcasted_iota(jnp.int32, (8, 128), 0)
@@ -157,8 +153,8 @@
         )
         spec_ref[parity] = waves.reshape(2, 8 * LAYERS, HALF)
 
-    def parameter(layer, block, row):
-        return jnp.broadcast_to(in_ref[pl.ds((layer * LAYERS + block) * 8 + row, 1), :], (8, 128))
+    def trait(layer, row):
+        return jnp.broadcast_to(trait_ref[8 * layer + row : 8 * layer + row + 1, :], (8, 128))
 
     for parity in range(2):
         for tile in range(2):
@@ -178,7 +174,7 @@
             (cs, _), (ss, _) = both
             rise = [jnp.zeros((8, 128), F32)] * 2
             for layer in range(LAYERS):
-                sat = parameter(layer, 0, 6)
+                sat = trait(layer, 0)
                 (xc, yc, zc), (xs, ys, zs) = load(layer, cos_at), load(layer, sin_at)
                 along = (cs["x"] * xc + cs["y"] * ys, ss["x"] * xs - ss["y"] * yc)
                 for part, (a, z) in enumerate(zip(along, (zc, zs))):
@@ -196,9 +192,9 @@
                     psi.append(keep_ref[layer, part, 0] + fall[part])
                     chi.append(keep_ref[layer, part, 1] - fall[part])
                     fall[part] = sym["step"] * fall[part] + keep_ref[layer, part, 2]
-                stiff = parameter(layer, 0, 7)
-                below = RKKY_STRENGTH * parameter(layer, 1, 6) if layer > 0 else None
-                above = RKKY_STRENGTH * parameter(layer, 1, 7) if layer < LAYERS - 1 else None
+                stiff = trait(layer, 1)
+                below = RKKY_STRENGTH * trait(layer, 2) if layer > 0 else None
+                above = RKKY_STRENGTH * trait(layer, 3) if layer < LAYERS - 1 else None
                 for part, (sym, at) in enumerate(both):
                     here = load(layer, at)
                     cross = cs["y"] * psi[1] if part == 0 else -ss["y"] * psi[0]
@@ -221,7 +217,7 @@
                     rise = jnp.zeros((8, 128), F32)
                     fall = rise
                     for layer in range(LAYERS):
-                        sat = parameter(layer, 0, 6)
+                        sat = trait(layer, 0)
                         x, y, _ = load(layer, at)
                         e = sat * (sym["top_x"] * x + sym["top_y"] * y)
                         top_ref[layer, 0] = (1.0 - sym["self_z"]) * e + rise
@@ -268,7 +264,7 @@
     lax.fori_loop(0, LAYERS, scatter, 0)
 
 
-def torque_kernel(damping_ref, magnet_ref, in_ref, high_ref, low_ref, out_ref):
+def finish(damping, magnet_ref, in_ref, high_ref, low_ref, out_ref):
     low_half = lane_low((DEVICES, 128))
     first = lax.broadcasted_iota(jnp.int32, (DEVICES, 128), 0) == 0
     parts = []
@@ -286,7 +282,6 @@
         sine = jnp.concatenate([jnp.where(low_half, x_two, -one), -up], axis=1)
         waves = jnp.concatenate([cosine, sine], axis=0)
         parts.append(product(split(waves), (high_ref[slot], low_ref[slot]), TN))
-    damping = damping_ref[0]
     factor = -1.0 / (1.0 + damping * damping)
     for far in range(2):
         at = slice(HALF * far, HALF * far + HALF)
@@ -299,41 +294,122 @@
             out_ref[ROWS * c : ROWS * c + ROWS, at] = factor * (p[c] + damping * relax)
 
 
-def call(kernel, out, scratch, inputs, smem):
-    spaces = [pltpu.SMEM] * smem + [pltpu.VMEM] * (len(inputs) - smem)
-    return pl.pallas_call(
+def kernel(
+    sat_ref,
+    stiff_ref,
+    damping_ref,
+    sign_ref,
+    magnet_ref,
+    high_ref,
+    low_ref,
+    out_ref,
+    send_one,
+    recv_one,
+    send_two,
+    recv_two,
+    trait_ref,
+    spec_ref,
+    field_ref,
+    keep_ref,
+    top_ref,
+    send_sems,
+    recv_sems,
+    ready,
+):
+    layer, row = lax.axis_index("layer"), lax.axis_index("row")
+    me = layer * LAYERS + row
+
+    def turned(index, by):
+        return jnp.bitwise_and(index + by, LAYERS - 1)
+
+    barrier = pltpu.get_barrier_semaphore()
+
+    def greet(step, carry):
+        for target in ((layer, turned(row, step)), (turned(layer, step), row)):
+            pl.semaphore_signal(barrier, inc=1, device_id=target, device_id_type=MESH)
+        return carry
+
+    lax.fori_loop(1, LAYERS, greet, 0)
+    kinds = lax.broadcasted_iota(jnp.int32, (8, 128), 0)
+    traits = jnp.where(kinds == 0, sat_ref[0], stiff_ref[0])
+    traits = jnp.where(kinds == 2, sign_ref[0, 0].astype(F32), traits)
+    traits = jnp.where(kinds == 3, sign_ref[0, 1].astype(F32), traits)
+    own_trait = pl.ds(pl.multiple_of(8 * layer, 8), 8)
+    trait_ref[own_trait, :] = traits
+    forward_x(magnet_ref, high_ref, low_ref, send_one, 0)
+    pl.semaphore_wait(barrier, 2 * (LAYERS - 1))
+
+    def vouch(step, carry):
+        target = (layer, turned(row, step))
+        pl.semaphore_signal(ready, inc=1, device_id=target, device_id_type=MESH)
+        return carry
+
+    lax.fori_loop(1, LAYERS, vouch, 0)
+    forward_x(magnet_ref, high_ref, low_ref, send_one, 1)
+    pl.semaphore_wait(ready, LAYERS - 1)
+
+    def tell(step, carry):
+        pltpu.make_async_remote_copy(
+            src_ref=trait_ref.at[own_trait],
+            dst_ref=trait_ref.at[own_trait],
+            send_sem=send_sems.at[2],
+            recv_sem=recv_sems.at[2],
+            device_id=(turned(layer, step), row),
+            device_id_type=MESH,
+        ).start()
+        return carry
+
+    lax.fori_loop(1, LAYERS, tell, 0)
+
+    def exchange(source, target, index):
+        def push(step, carry):
+            other = jnp.bitwise_and(me + step, DEVICES - 1)
+            pltpu.make_async_remote_copy(
+                src_ref=source.at[pl.ds(pl.multiple_of(8 * other, 8), USED)],
+                dst_ref=target.at[pl.ds(pl.multiple_of(8 * me, 8), USED)],
+                send_sem=send_sems.at[index],
+                recv_sem=recv_sems.at[index],
+                device_id=(jnp.right_shift(other, 4), jnp.bitwise_and(other, LAYERS - 1)),
+                device_id_type=MESH,
+            ).start()
+            return carry
+
+        lax.fori_loop(1, DEVICES, push, 0)
+        mine = pl.ds(pl.multiple_of(8 * me, 8), 8)
+        target[mine, :] = source[mine, :]
+        drain(source, target, index, USED * (DEVICES - 1))
+
+    def drain(source, target, index, count):
+        every = pl.ds(0, count)
+        pltpu.make_async_copy(source.at[every], source.at[every], send_sems.at[index]).wait()
+        pltpu.make_async_copy(target.at[every], target.at[every], recv_sems.at[index]).wait()
+
+    exchange(send_one, recv_one, 0)
+    drain(trait_ref, trait_ref, 2, 8 * (LAYERS - 1))
+    couple(
+        recv_one, high_ref, low_ref, send_two, trait_ref, spec_ref, field_ref, keep_ref, top_ref
+    )
+    exchange(send_two, recv_two, 1)
+    finish(damping_ref[0], magnet_ref, recv_two, high_ref, low_ref, out_ref)
+
+
+def on_device(magnet, saturation, stiffness, damping, interface_sign):
+    flat = magnet.reshape(3 * ROWS, N)
+    spaces = [pltpu.SMEM] * 4 + [pltpu.VMEM] * 3
+    buffer, spectrum = (8 * DEVICES, 128), (2, 2, 8 * LAYERS, HALF)
+    shapes = [buffer] * 4 + [(8 * LAYERS, 128), spectrum, spectrum]
+    shapes += [(LAYERS, 2, 3, 8, 128), (LAYERS, 2, 8, 128)]
+    torque = pl.pallas_call(
         kernel,
-        out_shape=jax.ShapeDtypeStruct(out, F32),
+        out_shape=jax.ShapeDtypeStruct(flat.shape, F32),
         in_specs=[pl.BlockSpec(memory_space=space) for space in spaces],
         out_specs=pl.BlockSpec(memory_space=pltpu.VMEM),
-        scratch_shapes=[pltpu.VMEM(shape, F32) for shape in scratch],
-    )(*inputs)
-
-
-def exchange(blocks):
-    blocks = blocks.reshape(DEVICES, 8, 128)
-    blocks = lax.all_to_all(blocks, ("layer", "row"), split_axis=0, concat_axis=0, tiled=True)
-    return blocks.reshape(8 * DEVICES, 128)
-
-
-def on_device(magnet, saturation, stiffness, damping, interface_sign):
-    flat = magnet.reshape(3 * ROWS, N)
-    high, low = wave_tables()
-    buffer = (8 * DEVICES, 128)
-    waves = call(
-        forward_x_kernel, buffer, [], (saturation, stiffness, interface_sign, flat, high, low), 3
-    )
-    spectrum = (2, 2, 8 * LAYERS, HALF)
-    fields = call(
-        couple_kernel,
-        buffer,
-        [spectrum, spectrum, (LAYERS, 2, 3, 8, 128), (LAYERS, 2, 8, 128)],
-        (exchange(waves), high, low),
-        0,
-    )
-    torque = call(
-        torque_kernel, flat.shape, [], (damping, flat, exchange(fields), high, low), 1
-    )
+        scratch_shapes=[pltpu.VMEM(shape, F32) for shape in shapes]
+        + [pltpu.SemaphoreType.DMA((3,))] * 2
+        + [pltpu.SemaphoreType.REGULAR],
+        compiler_params=pltpu.CompilerParams(collective_id=0, has_side_effects=True),
+        name="torque",
+    )(saturation, stiffness, damping, interface_sign, flat, *wave_tables())
     return torque.reshape(magnet.shape)
 
 

time: 104 us -> 71 us (0.68)
  Pallas kernels: 17.1 us -> 66.8 us
  blocking collectives: 47.5 us -> 0 us
  waiting for transfers between devices: 31.1 us -> 0 us
  starting transfers between devices: 5.58 us -> 0 us
  local copies, waits for them, and re-layouts: 0.97 us -> 2.09 us
    pallas_call x3 -> x1, Pallas kernels: 17.1 us -> 66.8 us  [on_device(): pl.pallas_call(kernel, out_shape=jax.ShapeDtypeStruct(flat.shape, F32), i...]
    all_to_all x1 -> x0, blocking collectives: 47.5 us -> none  [exchange(): lax.all_to_all(blocks, ('layer', 'row'), split_axis=0, concat_axis=0, til...]
    all_to_all x1 -> x0, waiting for transfers between devices: 31.1 us -> none  [exchange(): lax.all_to_all(blocks, ('layer', 'row'), split_axis=0, concat_axis=0, til...]
    all_to_all x1 -> x0, starting transfers between devices: 5.58 us -> none  [exchange(): lax.all_to_all(blocks, ('layer', 'row'), split_axis=0, concat_axis=0, til...]
    unnamed x2 -> x1, local copies, waits for them, and re-layouts: 0.97 us -> 2.09 us
  transfers between devices with their start and end apart: 1 -> 0, of which waited for: 1 -> 0; matrix products, arithmetic and copies ran while one was open for 0% -> 0% of each run, Pallas kernels for 0% -> 0%
where the time goes in v1:
time: 71 us; the launch traced here: 70.8 us
  Pallas kernels  66.8 us (94%)
  local copies, waits for them, and re-layouts  2.09 us (3%)
  between operations  1.95 us (3%)
    pallas_call x1, Pallas kernels, on_device(): pl.pallas_call(kernel, out_shape=jax.ShapeDtypeStruct(flat.shape, F32), i...  66.8 us
    unnamed x1, local copies, waits for them, and re-layouts  2.09 us

profile of v1, /device:TPU:1, one launch (start us, length us, event | category | flops | bytes accessed | tf_op | source)
XLA Modules:
  0.0 70.8 jit_solution(4389592835748214953)
XLA Ops:
  1.9 66.8 %torque.1 = f32[192,1024]{1,0:T(8,128)} custom-call(f32[1]{0:T(128)S(6)} %copy.10.sat_ref, f32[1]{0:T(128)S(6)} %copy.11.stiff_ref, f32[1]{0:T(128)S(6)} %copy.12.damping_ref, s32[1,2]{1,0:T(1,128)} %sign_ref.1, f32[192,1024]{1,0:T(8,128)} %bitcast.5, bf16[2,512,512]{2,1,0:T(8,128)(2,1)} %constant.4.clone.high_ref, bf16[2,512,512]{2,1,0:T(8,128)(2,1)} %constant.5.clone.low_ref), custom_call_target="tpu_custom_call" | custom-call | tf_op jit(solution)/shard_map/torque/pallas_call | solution.py:402
  68.7 2.1 %copy.13 = f32[3,1,64,1024]{3,2,1,0:T(8,128)} copy(f32[3,1,64,1024]{3,2,1,0:T(8,128)} %bitcast.4) | data formatting | bytes 1572864

commit v2 on v1

v2 whole, which is shorter than its diff:
```python
import functools
import math

import jax
import jax.numpy as jnp
import numpy as np
from jax import lax
from jax.experimental import pallas as pl
from jax.experimental.pallas import tpu as pltpu
from jax.sharding import PartitionSpec as P

N = 1024
HALF = N // 2
BINS = N // 4
LAYERS = 16
ROWS = 64
DEVICES = 256
THICKNESS = 1.0
LAYER_PITCH = 1.5
RKKY_STRENGTH = 0.8
F32 = jnp.float32
BF16 = jnp.bfloat16
NT = (((1,), (1,)), ((), ()))
NN = (((1,), (0,)), ((), ()))
TN = (((0,), (0,)), ((), ()))
USED = 3
PAIRS = LAYERS // 2
BLOCKS = DEVICES // 2
TILE = (8, 128)
MESH = pl.DeviceIdType.MESH


def wave_tables():
    grid = np.arange(HALF)
    bins = np.arange(BINS)
    tables = []
    for parity in range(2):
        phase = (2 * bins[:, None] + parity) * grid[None, :] % N * (2.0 * np.pi / N)
        cosines, sines = np.cos(phase), np.sin(phase)
        if parity == 0:
            sines[0] = 1.0 - 2.0 * (grid % 2)
        tables.append(np.concatenate([cosines, sines], axis=0))
    exact = np.stack(tables)
    high = exact.astype(np.dtype(BF16))
    low = (exact - high.astype(np.float64)).astype(np.dtype(BF16))
    return jnp.asarray(high), jnp.asarray(low)


def split(value):
    high = value.astype(BF16)
    return high, (value - high.astype(F32)).astype(BF16)


def product(left, right, dims):
    (left_high, left_low), (right_high, right_low) = left, right
    dot = functools.partial(lax.dot_general, dimension_numbers=dims, preferred_element_type=F32)
    return dot(left_high, right_high) + (dot(left_high, right_low) + dot(left_low, right_high))


def lane_low(shape):
    return lax.broadcasted_iota(jnp.int32, shape, len(shape) - 1) < ROWS


def flat(ref):
    return ref.reshape(ref.shape[0] * 8, 128)


def forward_x(magnet_ref, high_ref, low_ref, out_ref, slot):
    left, right = magnet_ref[:, :HALF], magnet_ref[:, HALF:]
    low_half = lane_low((DEVICES, 128))
    folded = left - right if slot else left + right
    folded = jnp.concatenate([folded, folded[2 * ROWS :]], axis=0)
    waves = product((high_ref[slot], low_ref[slot]), split(folded), NT)
    cosine, sine = waves[:BINS], waves[BINS:]
    one, two = cosine[:, :128], sine[:, :128]
    if slot == 0:
        first = lax.broadcasted_iota(jnp.int32, (DEVICES, 128), 0) == 0
        x_one, x_two = jnp.where(first, two, one), jnp.where(first, one, two)
    else:
        x_one, x_two = one, two
    out = flat(out_ref)
    out[pl.ds(4 * slot, DEVICES, stride=8), :] = jnp.where(low_half, x_one, -two)
    out[pl.ds(4 * slot + 1, DEVICES, stride=8), :] = jnp.where(low_half, x_two, one)
    out[pl.ds(4 * slot + 2, DEVICES, stride=8), :] = jnp.where(
        low_half, -sine[:, 128:], cosine[:, 128:]
    )


def symbols(device, slot, parity, tile, sine):
    bin_y = 2 * (lax.broadcasted_iota(jnp.int32, TILE, 1) + 128 * tile) + parity
    if sine and parity == 0:
        bin_y = jnp.where(bin_y == 0, HALF, bin_y)
    bin_x = jnp.full(TILE, 2 * device + slot, jnp.int32)
    if slot == 0:
        word = lax.broadcasted_iota(jnp.int32, TILE, 0) % 2
        bin_x = jnp.where(device == 0, jnp.where(word == 0, HALF, 0), bin_x)
    top_x, top_y = bin_x == HALF, bin_y == HALF
    wave_x = bin_x.astype(F32) * (2.0 * math.pi / N)
    wave_y = bin_y.astype(F32) * (2.0 * math.pi / N)
    square = wave_x * wave_x + wave_y * wave_y
    anchor = square == 0.0
    norm = jnp.sqrt(jnp.where(anchor, 1.0, square))
    unit_x = jnp.where(anchor, 0.0, wave_x / norm)
    unit_y = jnp.where(anchor, 0.0, wave_y / norm)
    depth = THICKNESS * norm
    series = 1.0 / 5040.0
    for divisor in (-720.0, 120.0, -24.0, 6.0, -2.0, 1.0):
        series = series * depth + 1.0 / divisor
    ratio = jnp.where(depth < 0.25, series, (1.0 - jnp.exp(-depth)) / depth)
    self_z = jnp.where(anchor, 1.0, ratio)
    near = jnp.where(
        anchor, 0.0, 0.5 * depth * ratio * ratio * jnp.exp(-norm * (LAYER_PITCH - THICKNESS))
    )
    step = jnp.exp(-LAYER_PITCH * norm)
    bend = 2.0 * jnp.cos(wave_x) + 2.0 * jnp.cos(wave_y) - 4.0
    scale_x = jnp.where(jnp.logical_or(bin_x == 0, top_x), 1.0, 2.0)
    scale_y = jnp.where(jnp.logical_or(bin_y == 0, top_y), 1.0, 2.0)
    scale = scale_x * scale_y * (1.0 / (N * N))
    return dict(
        x=jnp.where(top_x, 0.0, unit_x),
        y=jnp.where(top_y, 0.0, unit_y),
        top_x=jnp.where(top_x, -unit_x, 0.0),
        top_y=jnp.where(top_y, unit_y, 0.0),
        self_z=self_z,
        near=near,
        step=step,
        double=step * step,
        bend=bend * scale,
        scale=scale,
    )


def pack_traits(trait_ref, pack_ref):
    low_rows = lax.broadcasted_iota(jnp.int32, TILE, 0) < 4
    for pair in range(PAIRS):
        for kind in range(4):
            low, high = (
                jnp.broadcast_to(trait_ref[layer, kind : kind + 1, :], TILE)
                for layer in (2 * pair, 2 * pair + 1)
            )
            if kind == 2 and pair == 0:
                low = jnp.zeros(TILE, F32)
            if kind == 3 and pair == PAIRS - 1:
                high = jnp.zeros(TILE, F32)
            value = jnp.where(low_rows, low, high)
            pack_ref[kind, pair] = RKKY_STRENGTH * value if kind > 1 else value


def couple(slot, in_ref, high_ref, low_ref, out_ref, pack_ref, spec_ref, field_ref, keep_ref):
    device = lax.axis_index("layer") * LAYERS + lax.axis_index("row")
    low_half = lane_low(TILE)
    rows = lax.broadcasted_iota(jnp.int32, TILE, 0)
    low_rows = rows < 4
    place = jnp.bitwise_and(rows, 3)
    zero = jnp.zeros(TILE, F32)

    def gather(pair, carry):
        at = pl.ds(pl.multiple_of(pair * 8, 8), 8)
        for group in range(4):
            plus, minus = [], []
            for block in (2 * group, 2 * group + 1):
                first = slot * BLOCKS + pair * LAYERS + block
                one, two = in_ref[first], in_ref[first + 8]
                plus.append(one + two)
                minus.append(one - two)
            for parity, (one, two) in enumerate((plus, minus)):
                columns = slice(128 * group, 128 * group + 128)
                spec_ref[parity, 0, at, columns] = jnp.where(low_half, one, pltpu.roll(two, 64, 1))
                spec_ref[parity, 1, at, columns] = jnp.where(low_half, pltpu.roll(one, 64, 1), two)
        return carry

    lax.fori_loop(0, PAIRS, gather, 0, unroll=2)
    for parity in range(2):
        waves = product(
            split(spec_ref[parity].reshape(2 * 8 * PAIRS, HALF)),
            (high_ref[parity], low_ref[parity]),
            NT,
        )
        spec_ref[parity] = waves.reshape(2, 8 * PAIRS, HALF)

    def turn(value):
        return pltpu.roll(value, 4, 0)

    for parity in range(2):
        for tile in range(2):
            both = [
                (
                    symbols(device, slot, parity, tile, sine),
                    slice(BINS * sine + 128 * tile, BINS * sine + 128 * tile + 128),
                )
                for sine in range(2)
            ]

            def load(pair, at):
                at_rows = slice(8 * pair, 8 * pair + 8)
                one, two = spec_ref[parity, 0, at_rows, at], spec_ref[parity, 1, at_rows, at]
                up = jnp.where(place == 0, pltpu.roll(one, 6, 0), pltpu.roll(two, 7, 0))
                return one, two, up

            (cs, cos_at), (ss, sin_at) = both
            rise, last = [zero, zero], [zero, zero]
            for pair in range(PAIRS):
                sat = pack_ref[0, pair]
                (xc, yc, zc), (xs, ys, zs) = load(pair, cos_at), load(pair, sin_at)
                along = (cs["x"] * xc + cs["y"] * ys, ss["x"] * xs - ss["y"] * yc)
                for part, (a, z) in enumerate(zip(along, (zc, zs))):
                    sym = both[part][0]
                    keep_ref[pair, part, 3] = z
                    a, z = sat * a, sat * z
                    up, down = sym["near"] * (a + z), sym["near"] * (a - z)
                    turned = turn(up)
                    if pair:
                        rise[part] = rise[part] + jnp.where(low_rows, 0.0, turned)
                    else:
                        rise[part] = jnp.where(low_rows, 0.0, turned)
                    keep_ref[pair, part, 0] = (1.0 - sym["self_z"]) * a + rise[part]
                    keep_ref[pair, part, 1] = sym["self_z"] * z + rise[part]
                    keep_ref[pair, part, 2] = down
                    rise[part] = (
                        sym["double"] * rise[part]
                        + sym["step"] * up
                        + jnp.where(low_rows, turned, 0.0)
                    )
            fall = [zero, zero]
            for pair in reversed(range(PAIRS)):
                psi, chi = [], []
                for part in range(2):
                    sym = both[part][0]
                    down = keep_ref[pair, part, 2]
                    turned = turn(down)
                    fall[part] = fall[part] + jnp.where(low_rows, turned, 0.0)
                    psi.append(keep_ref[pair, part, 0] + fall[part])
                    chi.append(keep_ref[pair, part, 1] - fall[part])
                    fall[part] = (
                        sym["double"] * fall[part]
                        + sym["step"] * down
                        + jnp.where(low_rows, 0.0, turned)
                    )
                stiff, below, above = (pack_ref[kind, pair] for kind in (1, 2, 3))
                at_rows = slice(8 * pair, 8 * pair + 8)

                def raw(which, part, at):
                    rows_of = slice(8 * which, 8 * which + 8)
                    one, two = (spec_ref[parity, half, rows_of, at] for half in range(2))
                    return one, two, keep_ref[which, part, 3]

                for part, (sym, at) in enumerate(both):
                    here = raw(pair, part, at)
                    before = raw(pair - 1, part, at) if pair else (zero,) * 3
                    after = raw(pair + 1, part, at) if pair < PAIRS - 1 else (zero,) * 3
                    cross = cs["y"] * psi[1] if part == 0 else -ss["y"] * psi[0]
                    field = (-sym["x"] * psi[part], cross, -chi[part])
                    hx, hy, hz = (
                        sym["scale"]
                        * (
                            f
                            + below * turn(jnp.where(low_rows, v, b))
                            + above * turn(jnp.where(low_rows, n, v))
                        )
                        + (stiff * sym["bend"]) * v
                        for f, v, b, n in zip(field, here, before, after)
                    )
                    field_ref[parity, 0, at_rows, at] = jnp.where(place < 2, hx, pltpu.roll(hz, 2, 0))
                    field_ref[parity, 1, at_rows, at] = jnp.where(place < 2, hy, pltpu.roll(hz, 1, 0))

            def top():
                for part, (sym, at) in enumerate(both):
                    rise, fall = zero, zero
                    for pair in range(PAIRS):
                        x, y, _ = load(pair, at)
                        e = pack_ref[0, pair] * (sym["top_x"] * x + sym["top_y"] * y)
                        move = sym["near"] * e
                        turned = turn(move)
                        rise = rise + jnp.where(low_rows, 0.0, turned)
                        keep_ref[pair, part, 0] = (1.0 - sym["self_z"]) * e + rise
                        keep_ref[pair, part, 1] = move
                        rise = (
                            sym["double"] * rise
                            + sym["step"] * move
                            + jnp.where(low_rows, turned, 0.0)
                        )
                    for pair in reversed(range(PAIRS)):
                        move = keep_ref[pair, part, 1]
                        turned = turn(move)
                        fall = fall + jnp.where(low_rows, turned, 0.0)
                        psi = sym["scale"] * (keep_ref[pair, part, 0] + fall)
                        fall = (
                            sym["double"] * fall
                            + sym["step"] * move
                            + jnp.where(low_rows, 0.0, turned)
                        )
                        at_rows = slice(8 * pair, 8 * pair + 8)
                        for half, key in enumerate(("top_x", "top_y")):
                            field_ref[parity, half, at_rows, at] -= jnp.where(
                                place < 2, sym[key] * psi, 0.0
                            )

            if parity == 0 and tile == 0:
                top()
            elif slot == 0:
                pl.when(device == 0)(top)

    for parity in range(2):
        spec_ref[parity] = product(
            split(field_ref[parity].reshape(2 * 8 * PAIRS, HALF)),
            (high_ref[parity], low_ref[parity]),
            NN,
        ).reshape(2, 8 * PAIRS, HALF)

    def scatter(pair, carry):
        at = pl.ds(pl.multiple_of(pair * 8, 8), 8)
        for group in range(4):
            columns = slice(128 * group, 128 * group + 128)
            even = [spec_ref[0, half, at, columns] for half in range(2)]
            odd = [spec_ref[1, half, at, columns] for half in range(2)]
            for far in range(2):
                one, two = (e - o if far else e + o for e, o in zip(even, odd))
                block = slot * BLOCKS + pair * LAYERS + 8 * far + 2 * group
                out_ref[block] = jnp.where(low_half, one, pltpu.roll(two, 64, 1))
                out_ref[block + 1] = jnp.where(low_half, pltpu.roll(one, 64, 1), two)
        return carry

    lax.fori_loop(0, PAIRS, scatter, 0, unroll=2)


def inverse_x(slot, in_ref, high_ref, low_ref):
    low_half = lane_low((DEVICES, 128))
    ref = flat(in_ref)
    one, two, up = (ref[pl.ds(4 * slot + row, DEVICES, stride=8), :] for row in range(3))
    if slot == 0:
        first = lax.broadcasted_iota(jnp.int32, (DEVICES, 128), 0) == 0
        x_one, x_two = jnp.where(first, two, one), jnp.where(first, one, two)
    else:
        x_one, x_two = one, two
    cosine = jnp.concatenate([jnp.where(low_half, x_one, two), pltpu.roll(up, 64, 1)], axis=1)
    sine = jnp.concatenate([jnp.where(low_half, x_two, -one), -up], axis=1)
    waves = jnp.concatenate([cosine, sine], axis=0)
    return product(split(waves), (high_ref[slot], low_ref[slot]), TN)


def relax(damping, magnet_ref, even_ref, odd, out_ref):
    for far in range(2):
        at = slice(HALF * far, HALF * far + HALF)
        field = even_ref[...] - odd if far else even_ref[...] + odd
        h = [field[ROWS * c : ROWS * c + ROWS] for c in range(3)]
        m = [magnet_ref[ROWS * c : ROWS * c + ROWS, at] for c in range(3)]
        p = [m[c - 2] * h[c - 1] - m[c - 1] * h[c - 2] for c in range(3)]
        for c in range(3):
            double = m[c - 2] * p[c - 1] - m[c - 1] * p[c - 2]
            out_ref[ROWS * c : ROWS * c + ROWS, at] = p[c] + damping * double


def kernel(
    sat_ref,
    stiff_ref,
    damping_ref,
    sign_ref,
    magnet_hbm,
    high_hbm,
    low_hbm,
    out_ref,
    magnet_ref,
    high_ref,
    low_ref,
    send_one,
    recv_one,
    send_two,
    recv_two,
    trait_ref,
    pack_ref,
    spec_ref,
    field_ref,
    keep_ref,
    even_ref,
    load_sems,
    send_sems,
    recv_sems,
    ready,
):
    layer, row = lax.axis_index("layer"), lax.axis_index("row")
    me = layer * LAYERS + row
    pair, odd_layer = layer // 2, lax.rem(layer, 2)
    home = pair * LAYERS + row

    def turned(index, by):
        return jnp.bitwise_and(index + by, LAYERS - 1)

    barrier = pltpu.get_barrier_semaphore()

    def greet(step, carry):
        for target in ((layer, turned(row, step)), (turned(layer, step), row)):
            pl.semaphore_signal(barrier, inc=1, device_id=target, device_id_type=MESH)
        return carry

    lax.fori_loop(1, LAYERS, greet, 0)
    loads = [
        pltpu.make_async_copy(source, target, load_sems.at[index])
        for index, (source, target) in enumerate(
            ((magnet_hbm, magnet_ref), (high_hbm, high_ref), (low_hbm, low_ref))
        )
    ]
    for load in loads:
        load.start()
    kinds = lax.broadcasted_iota(jnp.int32, TILE, 0)
    traits = jnp.where(kinds == 0, sat_ref[0], stiff_ref[0])
    traits = jnp.where(kinds == 2, sign_ref[0, 0].astype(F32), traits)
    trait_ref[layer] = jnp.where(kinds == 3, sign_ref[0, 1].astype(F32), traits)
    for load in loads:
        load.wait()
    forward_x(magnet_ref, high_ref, low_ref, send_one, 0)
    pl.semaphore_wait(barrier, 2 * (LAYERS - 1))

    def vouch(step, carry):
        target = (turned(layer, step), row)
        pl.semaphore_signal(ready, inc=1, device_id=target, device_id_type=MESH)
        return carry

    lax.fori_loop(1, LAYERS, vouch, 0)
    forward_x(magnet_ref, high_ref, low_ref, send_one, 1)
    pl.semaphore_wait(ready, LAYERS - 1)

    def push(source, target, index, device_id):
        pltpu.make_async_remote_copy(
            src_ref=source,
            dst_ref=target,
            send_sem=send_sems.at[index],
            recv_sem=recv_sems.at[index],
            device_id=device_id,
            device_id_type=MESH,
        ).start()

    def tell(step, carry):
        push(trait_ref.at[layer], trait_ref.at[layer], 4, (turned(layer, step), row))
        return carry

    def place_of(index):
        return jnp.right_shift(index, 4), jnp.bitwise_and(index, LAYERS - 1)

    def out_first(slot, parity):
        lands = recv_one.at[slot * BLOCKS + home, pl.ds(4 * parity, USED)]

        def step_to(step, carry):
            other = jnp.bitwise_and(me + step, DEVICES - 1)
            push(send_one.at[other, pl.ds(4 * slot, USED)], lands, slot, place_of(other))
            return carry

        lax.fori_loop(1, DEVICES, step_to, 0)
        recv_one[slot * BLOCKS + home, 4 * parity : 4 * parity + USED, :] = send_one[
            me, 4 * slot : 4 * slot + USED, :
        ]

    def out_second(slot, parity):
        lands = recv_two.at[me, pl.ds(4 * slot, USED)]
        for target in (parity, 1 - parity):

            def step_to(step, carry):
                block = jnp.bitwise_and(home + step, BLOCKS - 1)
                other, other_row = place_of(block)
                push(
                    send_two.at[slot * BLOCKS + block, pl.ds(4 * target, USED)],
                    lands,
                    2 + slot,
                    (2 * other + target, other_row),
                )
                return carry

            lax.fori_loop(1 if target == parity else 0, BLOCKS, step_to, 0)
        recv_two[me, 4 * slot : 4 * slot + USED, :] = send_two[
            slot * BLOCKS + home, 4 * parity : 4 * parity + USED, :
        ]

    def by_parity(function, slot):
        for parity in range(2):
            pl.when(odd_layer == parity)(functools.partial(function, slot, parity))

    def drain(ref, sems, index, count):
        every = ref.at[pl.ds(0, count), pl.ds(0, USED)]
        pltpu.make_async_copy(every, every, sems.at[index]).wait()

    def drain_traits(sems):
        every = trait_ref.at[pl.ds(0, LAYERS - 1)]
        pltpu.make_async_copy(every, every, sems.at[4]).wait()

    lax.fori_loop(1, LAYERS, tell, 0)
    for slot in range(2):
        by_parity(out_first, slot)
    drain_traits(recv_sems)
    pack_traits(trait_ref, pack_ref)
    for slot in range(2):
        drain(recv_one, recv_sems, slot, DEVICES - 1)
        couple(
            slot, recv_one, high_ref, low_ref, send_two, pack_ref, spec_ref, field_ref, keep_ref
        )
        by_parity(out_second, slot)
    drain(recv_two, recv_sems, 2, DEVICES - 1)
    even_ref[...] = inverse_x(0, recv_two, high_ref, low_ref)
    for slot in range(2):
        drain(send_one, send_sems, slot, DEVICES - 1)
        drain(send_two, send_sems, 2 + slot, DEVICES - 1)
    drain_traits(send_sems)
    drain(recv_two, recv_sems, 3, DEVICES - 1)
    odd = inverse_x(1, recv_two, high_ref, low_ref)
    relax(damping_ref[0], magnet_ref, even_ref, odd, out_ref)


def on_device(magnet, saturation, stiffness, damping, interface_sign):
    rows = magnet.reshape(3 * ROWS, N)
    spaces = [pltpu.SMEM] * 4 + [pl.ANY] * 3
    buffer, spectrum = (DEVICES, 8, 128), (2, 2, 8 * PAIRS, HALF)
    table = pltpu.VMEM((2, HALF, HALF), BF16)
    shapes = [buffer] * 4 + [(LAYERS, *TILE), (4, PAIRS, *TILE), spectrum, spectrum]
    shapes += [(PAIRS, 2, 4, *TILE), (DEVICES, HALF)]
    torque = pl.pallas_call(
        kernel,
        out_shape=jax.ShapeDtypeStruct(rows.shape, F32),
        in_specs=[pl.BlockSpec(memory_space=space) for space in spaces],
        out_specs=pl.BlockSpec(memory_space=pltpu.VMEM),
        scratch_shapes=[pltpu.VMEM(rows.shape, F32), table, table]
        + [pltpu.VMEM(shape, F32) for shape in shapes]
        + [pltpu.SemaphoreType.DMA((3,))]
        + [pltpu.SemaphoreType.DMA((5,))] * 2
        + [pltpu.SemaphoreType.REGULAR],
        compiler_params=pltpu.CompilerParams(collective_id=0, has_side_effects=True),
        name="torque",
    )(saturation, stiffness, damping, interface_sign, rows, *wave_tables())
    factor = -1.0 / (1.0 + damping * damping)
    return (torque * factor).reshape(magnet.shape)


def solution(mesh):
    in_specs = (P(None, "layer", "row", None), P("layer"), P("layer"), P("layer"), P("layer", None))
    out_specs = P(None, "layer", "row", None)
    return jax.shard_map(
        on_device, mesh=mesh, in_specs=in_specs, out_specs=out_specs, check_vma=False
    )
```

time: 71 us -> 60.2 us (0.85)
  Pallas kernels: 66.8 us -> 55.9 us
  other arithmetic: 0 us -> 2.1 us
  local copies, waits for them, and re-layouts: 2.09 us -> 0 us
    pallas_call x1, Pallas kernels: 66.8 us -> 55.9 us  [on_device(): pl.pallas_call(kernel, out_shape=jax.ShapeDtypeStruct(rows.shape, F32), i...]
    mul x0 -> x1, other arithmetic: none -> 2.1 us  [on_device(): return (torque * factor).reshape(magnet.shape)]
    unnamed x1 -> x0, local copies, waits for them, and re-layouts: 2.09 us -> none
where the time goes in v2:
time: 60.2 us; the launch traced here: 60 us
  Pallas kernels  55.9 us (93%)
  other arithmetic  2.1 us (3%)
  between operations  1.99 us (3%)
    pallas_call x1, Pallas kernels, on_device(): pl.pallas_call(kernel, out_shape=jax.ShapeDtypeStruct(rows.shape, F32), i...  55.9 us
    mul x1, other arithmetic, on_device(): return (torque * factor).reshape(magnet.shape)  2.1 us

profile of v2, /device:TPU:1, one launch (start us, length us, event | category | flops | bytes accessed | tf_op | source)
XLA Modules:
  0.0 60.0 jit_solution(16865513077706906600)
XLA Ops:
  1.9 55.9 %torque.1 = f32[192,1024]{1,0:T(8,128)} custom-call(f32[1]{0:T(128)S(6)} %copy.9.sat_ref, f32[1]{0:T(128)S(6)} %copy.10.stiff_ref, f32[1]{0:T(128)S(6)} %copy.11.damping_ref, s32[1,2]{1,0:T(1,128)} %sign_ref.1, f32[192,1024]{1,0:T(8,128)} %bitcast.5, bf16[2,512,512]{2,1,0:T(8,128)(2,1)} %constant.8.clone.high_hbm, bf16[2,512,512]{2,1,0:T(8,128)(2,1)} %constant.9.clone.low_hbm), custom_call_target="tpu_custom_call" | custom-call | tf_op jit(solution)/shard_map/torque/pallas_call | solution.py:513
  57.9 2.1 %broadcast_multiply_fusion = f32[192,1024]{1,0:T(8,128)} fusion(f32[192,1024]{1,0:T(8,128)} %torque.1, f32[]{:T(128)} %bitcast.1), kind=kLoop, calls=%fused_computation | loop fusion | flops 196608 | bytes 1572868 | tf_op jit(solution)/shard_map/mul | solution.py:527

commit v3 on v2

--- a/solution.py
+++ b/solution.py
@@ -351,14 +351,18 @@
 
 
 def kernel(
+    sat_hbm,
+    stiff_hbm,
+    damping_hbm,
+    sign_hbm,
+    magnet_hbm,
+    high_hbm,
+    low_hbm,
+    out_ref,
     sat_ref,
     stiff_ref,
     damping_ref,
     sign_ref,
-    magnet_hbm,
-    high_hbm,
-    low_hbm,
-    out_ref,
     magnet_ref,
     high_ref,
     low_ref,
@@ -385,39 +389,39 @@
     def turned(index, by):
         return jnp.bitwise_and(index + by, LAYERS - 1)
 
+    def facing(step):
+        return jnp.bitwise_xor(layer, step)
+
     barrier = pltpu.get_barrier_semaphore()
 
     def greet(step, carry):
-        for target in ((layer, turned(row, step)), (turned(layer, step), row)):
+        for target in ((layer, turned(row, step)), (facing(step), row)):
             pl.semaphore_signal(barrier, inc=1, device_id=target, device_id_type=MESH)
         return carry
 
     lax.fori_loop(1, LAYERS, greet, 0)
+    sources = (sat_hbm, stiff_hbm, damping_hbm, sign_hbm, magnet_hbm, high_hbm, low_hbm)
+    targets = (sat_ref, stiff_ref, damping_ref, sign_ref, magnet_ref, high_ref, low_ref)
     loads = [
         pltpu.make_async_copy(source, target, load_sems.at[index])
-        for index, (source, target) in enumerate(
-            ((magnet_hbm, magnet_ref), (high_hbm, high_ref), (low_hbm, low_ref))
-        )
+        for index, (source, target) in enumerate(zip(sources, targets))
     ]
     for load in loads:
         load.start()
+    pl.semaphore_wait(barrier, 2 * (LAYERS - 1))
+
+    def vouch(step, carry):
+        target = (facing(step), row)
+        pl.semaphore_signal(ready.at[step], inc=1, device_id=target, device_id_type=MESH)
+        return carry
+
+    lax.fori_loop(1, LAYERS, vouch, 0)
+    for load in loads:
+        load.wait()
     kinds = lax.broadcasted_iota(jnp.int32, TILE, 0)
     traits = jnp.where(kinds == 0, sat_ref[0], stiff_ref[0])
-    traits = jnp.where(kinds == 2, sign_ref[0, 0].astype(F32), traits)
-    trait_ref[layer] = jnp.where(kinds == 3, sign_ref[0, 1].astype(F32), traits)
-    for load in loads:
-        load.wait()
-    forward_x(magnet_ref, high_ref, low_ref, send_one, 0)
-    pl.semaphore_wait(barrier, 2 * (LAYERS - 1))
-
-    def vouch(step, carry):
-        target = (turned(layer, step), row)
-        pl.semaphore_signal(ready, inc=1, device_id=target, device_id_type=MESH)
-        return carry
-
-    lax.fori_loop(1, LAYERS, vouch, 0)
-    forward_x(magnet_ref, high_ref, low_ref, send_one, 1)
-    pl.semaphore_wait(ready, LAYERS - 1)
+    traits = jnp.where(kinds == 2, sign_ref[0].astype(F32), traits)
+    trait_ref[layer] = jnp.where(kinds == 3, sign_ref[1].astype(F32), traits)
 
     def push(source, target, index, device_id):
         pltpu.make_async_remote_copy(
@@ -430,7 +434,7 @@
         ).start()
 
     def tell(step, carry):
-        push(trait_ref.at[layer], trait_ref.at[layer], 4, (turned(layer, step), row))
+        push(trait_ref.at[layer], trait_ref.at[layer], 4, (facing(step), row))
         return carry
 
     def place_of(index):
@@ -439,12 +443,21 @@
     def out_first(slot, parity):
         lands = recv_one.at[slot * BLOCKS + home, pl.ds(4 * parity, USED)]
 
-        def step_to(step, carry):
-            other = jnp.bitwise_and(me + step, DEVICES - 1)
-            push(send_one.at[other, pl.ds(4 * slot, USED)], lands, slot, place_of(other))
+        def to_row(other, step, carry):
+            other_row = turned(row, step)
+            source = send_one.at[other * LAYERS + other_row, pl.ds(4 * slot, USED)]
+            push(source, lands, slot, (other, other_row))
             return carry
 
-        lax.fori_loop(1, DEVICES, step_to, 0)
+        lax.fori_loop(1, LAYERS, functools.partial(to_row, layer), 0, unroll=5)
+
+        def to_layer(step, carry):
+            if slot == 0:
+                pl.semaphore_wait(ready.at[step], 1)
+            other = facing(step)
+            return lax.fori_loop(0, LAYERS, functools.partial(to_row, other), carry, unroll=4)
+
+        lax.fori_loop(1, LAYERS, to_layer, 0)
         recv_one[slot * BLOCKS + home, 4 * parity : 4 * parity + USED, :] = send_one[
             me, 4 * slot : 4 * slot + USED, :
         ]
@@ -464,7 +477,9 @@
                 )
                 return carry
 
-            lax.fori_loop(1 if target == parity else 0, BLOCKS, step_to, 0)
+            if target == parity:
+                lax.fori_loop(1, 4, step_to, 0, unroll=3)
+            lax.fori_loop(4 if target == parity else 0, BLOCKS, step_to, 0, unroll=4)
         recv_two[me, 4 * slot : 4 * slot + USED, :] = send_two[
             slot * BLOCKS + home, 4 * parity : 4 * parity + USED, :
         ]
@@ -481,9 +496,11 @@
         every = trait_ref.at[pl.ds(0, LAYERS - 1)]
         pltpu.make_async_copy(every, every, sems.at[4]).wait()
 
+    forward_x(magnet_ref, high_ref, low_ref, send_one, 0)
     lax.fori_loop(1, LAYERS, tell, 0)
-    for slot in range(2):
-        by_parity(out_first, slot)
+    by_parity(out_first, 0)
+    forward_x(magnet_ref, high_ref, low_ref, send_one, 1)
+    by_parity(out_first, 1)
     drain_traits(recv_sems)
     pack_traits(trait_ref, pack_ref)
     for slot in range(2):
@@ -505,7 +522,6 @@
 
 def on_device(magnet, saturation, stiffness, damping, interface_sign):
     rows = magnet.reshape(3 * ROWS, N)
-    spaces = [pltpu.SMEM] * 4 + [pl.ANY] * 3
     buffer, spectrum = (DEVICES, 8, 128), (2, 2, 8 * PAIRS, HALF)
     table = pltpu.VMEM((2, HALF, HALF), BF16)
     shapes = [buffer] * 4 + [(LAYERS, *TILE), (4, PAIRS, *TILE), spectrum, spectrum]
@@ -513,16 +529,19 @@
     torque = pl.pallas_call(
         kernel,
         out_shape=jax.ShapeDtypeStruct(rows.shape, F32),
-        in_specs=[pl.BlockSpec(memory_space=space) for space in spaces],
+        in_specs=[pl.BlockSpec(memory_space=pltpu.HBM)] * 7,
         out_specs=pl.BlockSpec(memory_space=pltpu.VMEM),
-        scratch_shapes=[pltpu.VMEM(rows.shape, F32), table, table]
+        scratch_shapes=[pltpu.SMEM((1,), F32)] * 3
+        + [pltpu.SMEM((2,), jnp.int32), pltpu.VMEM(rows.shape, F32), table, table]
         + [pltpu.VMEM(shape, F32) for shape in shapes]
-        + [pltpu.SemaphoreType.DMA((3,))]
+        + [pltpu.SemaphoreType.DMA((7,))]
         + [pltpu.SemaphoreType.DMA((5,))] * 2
-        + [pltpu.SemaphoreType.REGULAR],
-        compiler_params=pltpu.CompilerParams(collective_id=0, has_side_effects=True),
+        + [pltpu.SemaphoreType.REGULAR((LAYERS,))],
+        compiler_params=pltpu.CompilerParams(
+            collective_id=0, has_side_effects=True, vmem_limit_bytes=53 * 1024 * 1024
+        ),
         name="torque",
-    )(saturation, stiffness, damping, interface_sign, rows, *wave_tables())
+    )(saturation, stiffness, damping, interface_sign.reshape(2), rows, *wave_tables())
     factor = -1.0 / (1.0 + damping * damping)
     return (torque * factor).reshape(magnet.shape)
 

time: 60.2 us -> 56.1 us (0.932)
  Pallas kernels: 55.9 us -> 52.3 us
  other arithmetic: 2.1 us -> 0.95 us
  local copies, waits for them, and re-layouts: 0 us -> 0.65 us
    pallas_call x1, Pallas kernels: 55.9 us -> 52.3 us  [on_device(): pl.pallas_call(kernel, out_shape=jax.ShapeDtypeStruct(rows.shape, F32), i...]
    mul x1, other arithmetic: 2.1 us -> 0.95 us  [on_device(): return (torque * factor).reshape(magnet.shape)]
    unnamed x0 -> x2, local copies, waits for them, and re-layouts: none -> 0.65 us
where the time goes in v3:
time: 56.1 us; the launch traced here: 55.9 us
  Pallas kernels  52.3 us (93%)
  between operations  2 us (4%)
  other arithmetic  0.95 us (2%)
  local copies, waits for them, and re-layouts  0.65 us (1%)
    pallas_call x1, Pallas kernels, on_device(): pl.pallas_call(kernel, out_shape=jax.ShapeDtypeStruct(rows.shape, F32), i...  52.3 us

profile of v3, /device:TPU:1, one launch (start us, length us, event | category | flops | bytes accessed | tf_op | source)
XLA Modules:
  0.0 55.9 jit_solution(9404771151393469125)
XLA Ops:
  1.9 0.0 copy-start
  2.0 0.6 %copy-done = s32[1,2]{1,0:T(1,128)S(1)} copy-done((s32[1,2]{1,0:T(1,128)S(1)}, s32[1,2]{1,0:T(1,128)}, u32[]{:S(2)}) %copy-start) | copy-done | bytes 32
  2.6 52.3 %torque.1 = f32[192,1024]{1,0:T(8,128)S(1)} custom-call(f32[1]{0:T(128)S(6)} %copy.9.sat_hbm, f32[1]{0:T(128)S(6)} %copy.10.stiff_hbm, f32[1]{0:T(128)S(6)} %copy.11.damping_hbm, s32[2]{0:T(128)S(1)} %bitcast.6, f32[192,1024]{1,0:T(8,128)} %bitcast.7, bf16[2,512,512]{2,1,0:T(8,128)(2,1)} %constant.8.clone.high_hbm, bf16[2,512,512]{2,1,0:T(8,128)(2,1)} %constant.9.clone.low_hbm), custom_call_target="tpu_custom_call" | custom-call | tf_op jit(solution)/shard_map/torque/pallas_call | solution.py:529
  55.0 1.0 %broadcast_multiply_fusion = f32[192,1024]{1,0:T(8,128)} fusion(f32[192,1024]{1,0:T(8,128)S(1)} %torque.1, f32[]{:T(128)} %bitcast.2), kind=kLoop, calls=%fused_computation | loop fusion | flops 196608 | bytes 1572868 | tf_op jit(solution)/shard_map/mul | solution.py:546
Async XLA Ops:
  1.9 0.7 %copy-start = (s32[1,2]{1,0:T(1,128)S(1)}, s32[1,2]{1,0:T(1,128)}, u32[]{:S(2)}) copy-start(s32[1,2]{1,0:T(1,128)} %param.11) | copy-start | bytes 28

commit v4 on v3

--- a/solution.py
+++ b/solution.py
@@ -339,6 +339,7 @@
 
 
 def relax(damping, magnet_ref, even_ref, odd, out_ref):
+    factor = -1.0 / jnp.full((1, 1), 1.0 + damping * damping, F32)
     for far in range(2):
         at = slice(HALF * far, HALF * far + HALF)
         field = even_ref[...] - odd if far else even_ref[...] + odd
@@ -347,7 +348,7 @@
         p = [m[c - 2] * h[c - 1] - m[c - 1] * h[c - 2] for c in range(3)]
         for c in range(3):
             double = m[c - 2] * p[c - 1] - m[c - 1] * p[c - 2]
-            out_ref[ROWS * c : ROWS * c + ROWS, at] = p[c] + damping * double
+            out_ref[ROWS * c : ROWS * c + ROWS, at] = factor * (p[c] + damping * double)
 
 
 def kernel(
@@ -500,6 +501,7 @@
     lax.fori_loop(1, LAYERS, tell, 0)
     by_parity(out_first, 0)
     forward_x(magnet_ref, high_ref, low_ref, send_one, 1)
+    drain(send_one, send_sems, 0, DEVICES - 1)
     by_parity(out_first, 1)
     drain_traits(recv_sems)
     pack_traits(trait_ref, pack_ref)
@@ -512,7 +514,8 @@
     drain(recv_two, recv_sems, 2, DEVICES - 1)
     even_ref[...] = inverse_x(0, recv_two, high_ref, low_ref)
     for slot in range(2):
-        drain(send_one, send_sems, slot, DEVICES - 1)
+        if slot:
+            drain(send_one, send_sems, slot, DEVICES - 1)
         drain(send_two, send_sems, 2 + slot, DEVICES - 1)
     drain_traits(send_sems)
     drain(recv_two, recv_sems, 3, DEVICES - 1)
@@ -542,8 +545,7 @@
         ),
         name="torque",
     )(saturation, stiffness, damping, interface_sign.reshape(2), rows, *wave_tables())
-    factor = -1.0 / (1.0 + damping * damping)
-    return (torque * factor).reshape(magnet.shape)
+    return torque.reshape(magnet.shape)
 
 
 def solution(mesh):

time: 56.1 us -> 55.8 us (level)
  other arithmetic: 0.95 us -> 0 us
  local copies, waits for them, and re-layouts: 0.65 us -> 1.53 us
    mul x1 -> x0, other arithmetic: 0.95 us -> none  [on_device(): return (torque * factor).reshape(magnet.shape)]
    unnamed x2 -> x3, local copies, waits for them, and re-layouts: 0.65 us -> 1.53 us
where the time goes in v4:
time: 55.8 us; the launch traced here: 55.6 us
  Pallas kernels  52.1 us (93%)
  between operations  1.96 us (4%)
  local copies, waits for them, and re-layouts  1.53 us (3%)
    pallas_call x1, Pallas kernels, on_device(): pl.pallas_call(kernel, out_shape=jax.ShapeDtypeStruct(rows.shape, F32), i...  52.1 us
    unnamed x3, local copies, waits for them, and re-layouts  1.53 us

profile of v4, /device:TPU:1, one launch (start us, length us, event | category | flops | bytes accessed | tf_op | source)
XLA Modules:
  0.0 55.6 jit_solution(783752830783139518)
XLA Ops:
  1.9 0.0 copy-start
  2.0 0.6 %copy-done = s32[1,2]{1,0:T(1,128)S(1)} copy-done((s32[1,2]{1,0:T(1,128)S(1)}, s32[1,2]{1,0:T(1,128)}, u32[]{:S(2)}) %copy-start) | copy-done | bytes 32
  2.6 52.1 %torque.1 = f32[192,1024]{1,0:T(8,128)S(1)} custom-call(f32[1]{0:T(128)S(6)} %copy.10.sat_hbm, f32[1]{0:T(128)S(6)} %copy.11.stiff_hbm, f32[1]{0:T(128)S(6)} %copy.12.damping_hbm, s32[2]{0:T(128)S(1)} %bitcast.6, f32[192,1024]{1,0:T(8,128)} %bitcast.7, bf16[2,512,512]{2,1,0:T(8,128)(2,1)} %constant.4.clone.high_hbm, bf16[2,512,512]{2,1,0:T(8,128)(2,1)} %constant.5.clone.low_hbm), custom_call_target="tpu_custom_call" | custom-call | tf_op jit(solution)/shard_map/torque/pallas_call | solution.py:532
  54.8 0.9 %copy.13 = f32[3,1,64,1024]{3,2,1,0:T(8,128)} copy(f32[3,1,64,1024]{3,2,1,0:T(8,128)S(1)} %bitcast.5) | data formatting | bytes 1572864
Async XLA Ops:
  1.9 0.7 %copy-start = (s32[1,2]{1,0:T(1,128)S(1)}, s32[1,2]{1,0:T(1,128)}, u32[]{:S(2)}) copy-start(s32[1,2]{1,0:T(1,128)} %param.11) | copy-start | bytes 28
